TPU v7x, 512 devices: a whole 4x8x8 slice. The times are simulated.
512 devices in a mesh: shot: 64 (over x, y, core), det: 8 (over z).
Axes of the slice: x: 4, y: 8, z: 8, core: 2. Of those that a mesh axis runs over, the one named last changes fastest.
Arguments:
- events: int32 [65536, 8192], P('shot', 'det'), may hold values from 0 to 1, as said below
- pair_patches: int32 [8, 26, 2], P('det'), may hold values from 0 to 7, as said below
- pair_owners: int32 [8, 26, 2], P('det'), may hold values from 0 to 63, as said below
- triples: int32 [8, 256, 3], P('det'), may hold values from 0 to 1023, as said below
Outputs:
- intra_rates: float32 [64, 128, 128], P('det', 'shot')
- boundary_rates: float32 [8, 64, 2, 128, 128], P('det', 'shot')
- detector_load: float32 [64, 128], P(None, 'shot')
- triple_cumulant: float32 [8, 256], P('det')
Inputs may be any that keep to these rules, and one draw needn't show every extreme that they name: events[s, i] is 1 where detector i fired in shot s, else 0. `pair_patches`: row d lists 26 blocks of panel d, each naming two different patches of the panel; no two blocks name the same two patches. `pair_owners`: of the 52 owner entries of one panel, no shot index is named more than 2 times, and in every panel some index is named exactly 2 times. `triples`: each triple holds three different detector indices of the panel in increasing order.
All inputs are finite; a program needn't handle non-finite values.
Results may differ from a plain program's by a relative error of at most 0.0003.
Values sent between devices are 32-bit elements; how exact they have to be, the bound alone decides.
No kernel may reach another device: no remote copies, remote signals or barrier semaphores. Data moves between devices by JAX's collectives and lax.ppermute only.
A program may use at most 64 MiB of HBM per device.

v0:
```python
import jax
import jax.numpy as jnp
from jax import lax
from jax.sharding import Mesh
from jax.sharding import PartitionSpec as P

PB = 128
SHOT = ("shot_0", "shot_1", "shot_2")


def split_up(x, dim, count):
    before, after = (x.shape[:dim], x.shape[dim + 1 :])
    return jnp.moveaxis(x.reshape(*before, count, -1, *after), dim, 0)


def sum_at_owner(x, axis, dim):
    tiles = split_up(x, dim, lax.axis_size(axis))
    arrived = lax.all_to_all(tiles, axis, split_axis=0, concat_axis=0, tiled=True)
    return arrived.sum(axis=0)


def by_axis(x, axes):
    for axis in axes:
        x = lax.psum(x, axis)
    return x


def laid_out(tiles, dim):
    tiles = jnp.moveaxis(tiles, 0, dim)
    dims = tiles.shape
    return tiles.reshape(*dims[:dim], dims[dim] * dims[dim + 1], *dims[dim + 2 :])


def sent_to_all(x, axis):
    copies = jnp.broadcast_to(x, (lax.axis_size(axis), *x.shape))
    return lax.all_to_all(copies, axis, split_axis=0, concat_axis=0, tiled=True)


def gather_directly(x, axis, dim):
    return laid_out(sent_to_all(x, axis), dim)


def fit_rates(coincide, row_count, col_count, shot_total):
    inverse = 1.0 / shot_total
    joint_rate = coincide * inverse
    row_rate = row_count[..., :, None] * inverse
    col_rate = col_count[..., None, :] * inverse
    denominator = jnp.maximum(1.0 - 2.0 * row_rate - 2.0 * col_rate + 4.0 * joint_rate, 0.25)
    excess = (joint_rate - row_rate * col_rate) / denominator
    return 100.0 * (0.5 - 0.5 * jnp.sqrt(jnp.maximum(1.0 - 4.0 * excess, 0.04)))


def route_table(owner_row, shot_count, recv_slots):
    owner_ids = jnp.arange(shot_count, dtype=jnp.int32)
    hit = owner_row[None, :] == owner_ids[:, None]
    rank = jnp.cumsum(hit.astype(jnp.int32), axis=1) - 1
    slot_ids = jnp.arange(recv_slots, dtype=jnp.int32)
    chosen = hit[:, None, :] & (rank[:, None, :] == slot_ids[None, :, None])
    entry_pair = jnp.arange(owner_row.shape[0], dtype=jnp.int32) // 2
    pair_slot = jnp.sum(jnp.where(chosen, entry_pair[None, None, :], 0), axis=2)
    valid = jnp.any(chosen, axis=2).astype(jnp.float32)
    return (pair_slot, valid)


def local(events, pair_patches, pair_owners, triples):
    shot_dev, det_dev = events.shape
    shot_count = lax.axis_size(SHOT)
    shot_index = lax.axis_index(SHOT)
    shot_total = float(shot_dev * shot_count)
    inverse = 1.0 / shot_total
    patch_dev = det_dev // PB
    rows_own = PB // shot_count
    pair_count = pair_patches.shape[1]
    triple_count = triples.shape[1]
    recv_slots = max(2, 4 * pair_count // shot_count)
    bit_matrix = events.astype(jnp.bfloat16)
    patches = bit_matrix.reshape(shot_dev, patch_dev, PB)
    local_counts = jnp.sum(events, axis=0).astype(jnp.float32)
    triple_index = triples[0]
    picked = (
        jnp.take(events, triple_index.reshape(-1), axis=1)
        .astype(jnp.float32)
        .reshape(shot_dev, triple_count, 3)
    )
    first_bit = picked[:, :, 0]
    second_bit = picked[:, :, 1]
    third_bit = picked[:, :, 2]
    triple_terms = jnp.stack(
        [
            jnp.sum(first_bit * second_bit, axis=0),
            jnp.sum(first_bit * third_bit, axis=0),
            jnp.sum(second_bit * third_bit, axis=0),
            jnp.sum(first_bit * second_bit * third_bit, axis=0),
        ]
    )
    intra = jnp.einsum("sai,saj->aij", patches, patches, preferred_element_type=jnp.float32)
    pair_ends = pair_patches[0]
    first_columns = jnp.take(patches, pair_ends[:, 0], axis=1)
    second_columns = jnp.take(patches, pair_ends[:, 1], axis=1)
    cross = jnp.einsum(
        "spi,spj->pij", first_columns, second_columns, preferred_element_type=jnp.float32
    )
    joined = sum_at_owner(jnp.concatenate([intra, cross], axis=0), SHOT, 1)
    intra_share = joined[:patch_dev]
    pair_share = joined[patch_dev:]
    counts, triple_total = (by_axis(local_counts, SHOT), by_axis(triple_terms, SHOT))
    patch_counts = counts.reshape(patch_dev, PB)
    row_counts = lax.dynamic_slice_in_dim(patch_counts, shot_index * rows_own, rows_own, 1)
    intra_rates = fit_rates(intra_share, row_counts, patch_counts, shot_total)
    load_share = jnp.sum(intra_rates, axis=2)
    detector_load = gather_directly(load_share, "det", 0)
    pair_slot, valid = route_table(pair_owners[0].reshape(-1), shot_count, recv_slots)
    fitted = fit_rates(
        pair_share,
        jnp.take(row_counts, pair_ends[:, 0], axis=0),
        jnp.take(patch_counts, pair_ends[:, 1], axis=0),
        shot_total,
    )
    outgoing = jnp.take(fitted, pair_slot.reshape(-1), axis=0).reshape(
        shot_count, recv_slots, rows_own, PB
    )
    outgoing = outgoing * valid[:, :, None, None]
    incoming = lax.all_to_all(outgoing, SHOT, split_axis=0, concat_axis=2, tiled=True)
    boundary = incoming.reshape(recv_slots, PB, PB)
    moments = triple_total * inverse
    means = jnp.take(counts, triple_index.reshape(-1), axis=0).reshape(triple_count, 3) * inverse
    mean_first = means[:, 0]
    mean_second = means[:, 1]
    mean_third = means[:, 2]
    kappa = (
        moments[3]
        - moments[0] * mean_third
        - moments[1] * mean_second
        - moments[2] * mean_first
        + 2.0 * mean_first * mean_second * mean_third
    )
    triple_cumulant = 1000.0 * kappa
    return (intra_rates, boundary[None, None], detector_load, triple_cumulant[None])


def solution(mesh):
    torus = Mesh(
        mesh.devices.reshape(4, 8, 2, mesh.shape["det"]), ("shot_0", "shot_1", "shot_2", "det")
    )
    return jax.shard_map(
        local,
        mesh=torus,
        in_specs=(P(SHOT, "det"), P("det", None, None), P("det", None, None), P("det", None, None)),
        out_specs=(
            P("det", SHOT, None),
            P("det", SHOT, None, None, None),
            P(None, SHOT),
            P("det", None),
        ),
        check_vma=False,
    )
```

profile of v0, /device:TPU:6, one launch (start us, length us, event | category | flops | bytes accessed | tf_op | source)
XLA Modules:
  0.0 153.1 jit_solution(5718766093984803097)
XLA Ops:
  0.6 5.4 %copy.90 = s32[1024,1024]{0,1:T(8,128)} copy(s32[1024,1024]{1,0:T(8,128)} %param.6) | data formatting | bytes 8388608 | tf_op args[0]
  6.0 2.8 %convert_element_type.24 = bf16[1024,1024]{0,1:T(8,128)(2,1)S(1)} convert(s32[1024,1024]{0,1:T(8,128)} %copy.90) | non-fusion elementwise | flops 1048576 | bytes 6291456 | tf_op jit(solution)/shard_map/convert_element_type | solution.py:76
  8.8 1.3 copy-done
  10.1 0.7 fusion.24
  10.8 3.0 %copy.92 = bf16[1024,8,128]{2,0,1:T(8,128)(2,1)S(1)} copy(bf16[1024,8,128]{0,2,1:T(8,128)(2,1)} %bitcast.87) | data formatting | bytes 4194304 | tf_op jit(solution)/shard_map/reshape | solution.py:77
  13.9 4.6 %gather_fusion.6 = bf16[26,1024,128]{2,1,0:T(8,128)(2,1)} fusion(bf16[1024,8,128]{2,0,1:T(8,128)(2,1)S(1)} %copy.92, s32[1024]{0:T(1024)S(1)} %get-tuple-element.40), kind=kCustom, calls=%fused_computation.1.clone | custom fusion | bytes 13631592 | tf_op jit(solution)/shard_map/jit(_take)/gather | solution.py:99
  18.5 4.6 %gather_fusion.5 = bf16[26,1024,128]{2,1,0:T(8,128)(2,1)} fusion(bf16[1024,8,128]{2,0,1:T(8,128)(2,1)S(1)} %copy.92, s32[1024]{0:T(1024)S(1)} %get-tuple-element.41), kind=kCustom, calls=%fused_computation.clone | custom fusion | bytes 13631592 | tf_op jit(solution)/shard_map/jit(_take)/gather | solution.py:98
  23.1 7.4 %fusion = f32[26,128,128]{2,1,0:T(8,128)S(1)} fusion(bf16[26,1024,128]{2,1,0:T(8,128)(2,1)} %gather_fusion.6, bf16[26,1024,128]{2,1,0:T(8,128)(2,1)} %gather_fusion.5, pred[26]{0:T(512)(128)(4,1)S(1)} %get-tuple-element.36, pred[26]{0:T(512)(128)(4,1)S(1)} %get-tuple-element.22), kind=kOutput, calls=%fused_computation.7 | convolution fusion | flops 879230976 | bytes 15335476 | tf_op jit(solution)/shard_map/spi,spj->pij/dot_general | solution.py:100
  30.7 2.1 %copy.115 = f32[34,64,2,128]{3,2,0,1:T(2,128)} copy(f32[34,64,2,128]{3,2,1,0:T(2,128)S(1)} %bitcast.89) | data formatting | bytes 4456448 | tf_op jit(solution)/shard_map/reshape | solution.py:13
  32.8 11.1 %all-to-all-start = ((f32[64,34,2,128]{3,2,1,0:T(2,128)}), f32[64,34,2,128]{3,2,1,0:T(2,128)}, u32[]{:S(2)}, u32[]{:S(2)}) async-start(f32[64,34,2,128]{3,2,1,0:T(2,128)} %bitcast.83), calls=%async_computation | async-start | bytes 4456448 | tf_op jit(solution)/shard_map/all_to_all | solution.py:18
  43.9 2.5 %reduce_sum.73 = s32[1024]{0:T(1024)S(1)} reduce(s32[1024,1024]{1,0:T(8,128)} %param.6, s32[]{:T(128)} %constant.84.clone.1), dimensions={0}, to_apply=%region_1.0 | reduce | flops 1047552 | bytes 4198404 | tf_op jit(solution)/shard_map/reduce_sum | solution.py:78
  48.2 6.1 %gather_fusion.3 = s32[768,1024]{1,0:T(8,128)S(1)} fusion(s32[1024,1024]{0,1:T(8,128)} %copy.90, s32[1024]{0:T(1024)S(1)} %pad_clamp_fusion), kind=kCustom, calls=%fused_computation.5 | custom fusion | bytes 6294528 | tf_op jit(solution)/shard_map/jit(_take)/gather | solution.py:81
  54.4 3.1 %gather.34 = s32[1024,256,3]{0,2,1:T(4,128)} reshape(s32[1024,768]{0,1:T(8,128)S(1)} %bitcast.88) | data formatting | bytes 6291456 | tf_op jit(solution)/shard_map/jit(_take)/gather | solution.py:81
  57.4 3.4 %copy.110 = s32[1024,256,3]{1,0,2:T(8,128)S(1)} copy(s32[1024,256,3]{0,2,1:T(4,128)} %gather.34) | data formatting | bytes 6291456 | tf_op jit(solution)/shard_map/jit(_take)/gather | solution.py:81
  61.5 7.6 %all-reduce.1 = (f32[1024]{0:T(1024)S(1)}, f32[4,256]{1,0:T(4,128)S(1)}) all-reduce(f32[1024]{0:T(1024)S(1)} %convert_element_type.25, f32[4,256]{1,0:T(4,128)S(1)} %pad_maximum_fusion.1), channel_id=1, replica_groups=mesh['shot_0'=4,'shot_1'=8,'shot_2'=2,'det'=8] {'shot_0'}, use_global_device_ids=true, to_apply=%region_2.4 | all-reduce | flops 2048 | bytes 16384 | tf_op jit(solution)/shard_map/psum | solution.py:24
  69.1 35.5 %all-reduce = (f32[1024]{0:T(1024)S(1)}, f32[4,256]{1,0:T(4,128)S(1)}) all-reduce(f32[1024]{0:T(1024)S(1)} %get-tuple-element.14, f32[4,256]{1,0:T(4,128)S(1)} %get-tuple-element.15), channel_id=1, replica_groups=mesh['shot_0'=4,'shot_1'=8,'shot_2'=2,'det'=8] {'shot_1'}, use_global_device_ids=true, to_apply=%region_3.5 | all-reduce | flops 2048 | bytes 16384 | tf_op jit(solution)/shard_map/psum | solution.py:24
  104.6 2.7 %all-reduce.2 = (f32[1024]{0:T(1024)S(1)}, f32[4,256]{1,0:T(4,128)S(1)}) all-reduce(f32[1024]{0:T(1024)S(1)} %get-tuple-element.12, f32[4,256]{1,0:T(4,128)S(1)} %get-tuple-element.13), channel_id=1, replica_groups=mesh['shot_0'=4,'shot_1'=8,'shot_2'=2,'det'=8] {'shot_2'}, use_global_device_ids=true, to_apply=%region_4.6 | all-reduce | flops 2048 | bytes 16384 | tf_op jit(solution)/shard_map/psum | solution.py:24
  107.3 3.2 %gather_fusion.4 = f32[768]{0:T(1024)S(1)} fusion(f32[1024]{0:T(1024)S(1)} %get-tuple-element.16, s32[1024]{0:T(1024)S(1)} %pad_clamp_fusion), kind=kCustom, calls=%fused_computation.6 | custom fusion | bytes 9216 | tf_op jit(solution)/shard_map/jit(_take)/gather | solution.py:126
  110.7 0.6 gather_fusion.1
  111.3 0.6 gather_fusion
  112.2 2.3 %reduce_sum.72 = f32[34,2,128]{2,1,0:T(2,128)S(1)} reduce(f32[64,34,2,128]{3,2,1,0:T(2,128)} %all-to-all-done, f32[]{:T(128)} %constant.82.clone.1), dimensions={0}, to_apply=%region_0.2 | reduce | flops 548352 | bytes 2263044 | tf_op jit(solution)/shard_map/reduce_sum | solution.py:19
  114.5 0.7 fusion.23
  115.2 0.6 broadcast_in_dim.91
  115.8 10.3 %all-to-all-start.2 = ((f32[8,8,2]{1,2,0:T(2,128)}), f32[8,8,2]{1,2,0:T(2,128)S(1)}, u32[]{:S(2)}, u32[]{:S(2)}) async-start(f32[8,8,2]{1,2,0:T(2,128)} %broadcast_in_dim.91), calls=%async_computation.2 | async-start | bytes 16384 | tf_op jit(solution)/shard_map/all_to_all | solution.py:36
  126.3 0.7 gather_fusion.2
  127.0 1.0 select_multiply_fusion.1
  128.0 5.8 %all-to-all-done.2 = f32[8,8,2]{1,2,0:T(2,128)S(1)} async-done(((f32[8,8,2]{1,2,0:T(2,128)}), f32[8,8,2]{1,2,0:T(2,128)S(1)}, u32[]{:S(2)}, u32[]{:S(2)}) %all-to-all-start.2) | async-done | bytes 544 | tf_op jit(solution)/shard_map/all_to_all | solution.py:36
  133.8 9.7 %all-to-all-start.1 = ((f32[64,2,2,128]{3,2,1,0:T(2,128)}), f32[64,2,2,128]{3,2,1,0:T(2,128)S(1)}, u32[]{:S(2)}, u32[]{:S(2)}) async-start(f32[64,2,2,128]{3,2,1,0:T(2,128)} %select_multiply_fusion.1), calls=%async_computation.1 | async-start | bytes 262144 | tf_op jit(solution)/shard_map/all_to_all | solution.py:123
  143.8 0.6 fusion.17
  144.4 0.6 reshape.307
  145.0 7.3 %all-to-all-done.1 = f32[64,2,2,128]{3,2,1,0:T(2,128)S(1)} async-done(((f32[64,2,2,128]{3,2,1,0:T(2,128)}), f32[64,2,2,128]{3,2,1,0:T(2,128)S(1)}, u32[]{:S(2)}, u32[]{:S(2)}) %all-to-all-start.1) | async-done | bytes 131104 | tf_op jit(solution)/shard_map/all_to_all | solution.py:123
  152.4 0.7 copy.103
  (55 shorter events, 3.6 us)
Async XLA Ops:
  8.8 1.4 copy-start
  10.8 3.1 %copy-start.1 = (s32[1,26,2]{1,2,0:T(2,128)S(1)}, s32[1,26,2]{1,2,0:T(2,128)}, u32[]{:S(2)}) copy-start(s32[1,26,2]{1,2,0:T(2,128)} %param.7) | copy-start | bytes 628
  32.8 79.3 %all-to-all-start = ((f32[64,34,2,128]{3,2,1,0:T(2,128)}), f32[64,34,2,128]{3,2,1,0:T(2,128)}, u32[]{:S(2)}, u32[]{:S(2)}) async-start(f32[64,34,2,128]{3,2,1,0:T(2,128)} %bitcast.83), calls=%async_computation | async-start | bytes 4456448 | tf_op jit(solution)/shard_map/all_to_all | solution.py:18
  43.9 2.5 %copy-start.3 = (s32[1,26,2]{1,2,0:T(2,128)S(1)}, s32[1,26,2]{1,2,0:T(2,128)}, u32[]{:S(2)}) copy-start(s32[1,26,2]{1,2,0:T(2,128)} %param.8) | copy-start | bytes 628
  43.9 3.8 %copy-start.2 = (s32[1,256,3]{1,0,2:T(1,128)S(1)}, s32[1,256,3]{1,0,2:T(1,128)}, u32[]{:S(2)}) copy-start(s32[1,256,3]{1,0,2:T(1,128)} %param.9) | copy-start | bytes 9220
  115.8 18.0 %all-to-all-start.2 = ((f32[8,8,2]{1,2,0:T(2,128)}), f32[8,8,2]{1,2,0:T(2,128)S(1)}, u32[]{:S(2)}, u32[]{:S(2)}) async-start(f32[8,8,2]{1,2,0:T(2,128)} %broadcast_in_dim.91), calls=%async_computation.2 | async-start | bytes 16384 | tf_op jit(solution)/shard_map/all_to_all | solution.py:36
  133.8 18.5 %all-to-all-start.1 = ((f32[64,2,2,128]{3,2,1,0:T(2,128)}), f32[64,2,2,128]{3,2,1,0:T(2,128)S(1)}, u32[]{:S(2)}, u32[]{:S(2)}) async-start(f32[64,2,2,128]{3,2,1,0:T(2,128)} %select_multiply_fusion.1), calls=%async_computation.1 | async-start | bytes 262144 | tf_op jit(solution)/shard_map/all_to_all | solution.py:123
where the time goes:
time: 156 us; the launch traced here: 153 us
  blocking collectives  45.7 us (29%)
  local copies, waits for them, and re-layouts  42.5 us (27%)
  starting transfers between devices  31 us (20%)
  waiting for transfers between devices  13.2 us (8%)
  other arithmetic  11.5 us (7%)
  matrix products  8.11 us (5%)
    psum x3, blocking collectives, by_axis(): x = lax.psum(x, axis)  45.7 us
    gather x3, local copies, waits for them, and re-layouts, local(): jnp.take(events, triple_index.reshape(-1), axis=1).astype(jnp.float32)  12.6 us
    all_to_all x1, starting transfers between devices, sum_at_owner(): lax.all_to_all(tiles, axis, split_axis=0, concat_axis=0, tiled=True)  11.1 us
    all_to_all x1, starting transfers between devices, sent_to_all(): return lax.all_to_all(copies, axis, split_axis=0, concat_axis=0, tiled=True)  10.3 us
    all_to_all x1, starting transfers between devices, local(): lax.all_to_all(outgoing, SHOT, split_axis=0, concat_axis=2, tiled=True)  9.68 us
    dot_general x1, matrix products, local(): jnp.einsum('spi,spj->pij', first_columns, second_columns, preferred_eleme...  7.41 us
    all_to_all x1, waiting for transfers between devices, local(): lax.all_to_all(outgoing, SHOT, split_axis=0, concat_axis=2, tiled=True)  7.35 us
    unnamed x11, local copies, waits for them, and re-layouts  6.97 us
  transfers between devices with their start and end apart: 3, of which 2 were waited for; matrix products, arithmetic and copies ran while one was open for 17% of the time, Pallas kernels for 0%

commit v1 on v0

v1 whole, which is shorter than its diff:
```python
import functools

import jax
import jax.numpy as jnp
from jax import lax
from jax.experimental import pallas as pl
from jax.experimental.pallas import tpu as pltpu
from jax.sharding import Mesh
from jax.sharding import PartitionSpec as P

PB = 128
SHOT = ("shot_0", "shot_1", "shot_2")


def fit(joint, rows, cols, inverse):
    u = joint * inverse
    x = rows * inverse
    y = cols * inverse
    den = jnp.maximum(1.0 - 2.0 * x - 2.0 * y + 4.0 * u, 0.25)
    q = (u - x * y) / den
    return 100.0 * (0.5 - 0.5 * jnp.sqrt(jnp.maximum(1.0 - 4.0 * q, 0.04)))


def iota(shape, dim):
    return lax.broadcasted_iota(jnp.int32, shape, dim)


def ordered(pairs, k):
    return jnp.minimum(pairs[0, k], pairs[1, k]), jnp.maximum(pairs[0, k], pairs[1, k])


def count_kernel(
    core, pairs, triple_rows, events, keep, send,
    raw, bits, flipped, grams, picker, sems,
    *, chunks, patches, pair_count, near, far, rows_own, vector_rows,
):
    shots, dets = raw.shape
    step = shots // chunks
    triple_count = triple_rows.shape[2]
    halves = triple_count // PB
    copies = [
        pltpu.make_async_copy(events.at[pl.ds(i * step, step)], raw.at[pl.ds(i * step, step)], sems.at[i])
        for i in range(chunks)
    ]
    for copy in copies:
        copy.start()
    detector = iota((dets, triple_count), 0)
    for m in range(3):
        hit = detector == triple_rows[m]
        picker[:, m * triple_count : (m + 1) * triple_count] = jnp.where(hit, 1.0, 0.0).astype(jnp.bfloat16)
    counts = jnp.zeros((1, dets), jnp.float32)
    sums = [jnp.zeros((1, triple_count), jnp.float32) for _ in range(7)]
    wide = 2 * PB

    def add_grams(first, last, fresh):
        for j in range(dets // wide):
            height = (j + 1) * wide
            panel = jnp.dot(
                flipped[:height, first:last],
                bits[first:last, j * wide : (j + 1) * wide],
                preferred_element_type=jnp.float32,
            )
            for h in range(2):
                span = slice((2 * j + h) * dets, (2 * j + h) * dets + height)
                part = panel[:, h * PB : (h + 1) * PB]
                grams[span, :] = part if fresh else grams[span, :] + part

    for i in range(chunks):
        copies[i].wait()
        span = slice(i * step, (i + 1) * step)
        values = raw[span, :].astype(jnp.float32)
        counts += jnp.sum(values, axis=0, keepdims=True)
        narrow = values.astype(jnp.bfloat16)
        bits[span, :] = narrow
        flipped[:, span] = narrow.T
        picked = jnp.dot(narrow, picker[...], preferred_element_type=jnp.float32)
        a, b, c = (picked[:, m * triple_count : (m + 1) * triple_count] for m in range(3))
        ab = a * b
        terms = (ab, a * c, b * c, ab * c, a, b, c)
        sums = [s + jnp.sum(t, axis=0, keepdims=True) for s, t in zip(sums, terms, strict=True)]
        if i == chunks // 2 - 1:
            add_grams(0, shots // 2, True)
    add_grams(shots // 2, shots, False)
    part = far * rows_own + vector_rows
    lines = [counts[:, p * PB : (p + 1) * PB] for p in range(patches)]
    lines += [s[:, h * PB : (h + 1) * PB] for s in sums for h in range(halves)]
    lines += [jnp.zeros((1, PB), jnp.float32)] * (vector_rows - len(lines))
    vectors = jnp.concatenate(lines, axis=0)
    for target in (keep, send):
        for x in range(near):
            target[(x + 1) * part - vector_rows : (x + 1) * part, :] = vectors
    mine = core[0]

    def place(block, start):
        for target, side in ((keep, mine), (send, 1 - mine)):
            for x in range(near):
                for r in range(2):
                    rows = grams[pl.ds(start + 4 * far * x + 2 * side + r, far, stride=4), :]
                    target[pl.ds(x * part + 2 * block + r, far, stride=rows_own), :] = rows

    for p in range(patches):
        place(p, p * dets + p * PB)

    def pair(k, carry):
        low, high = ordered(pairs, k)
        place(patches + k, high * dets + low * PB)
        return carry

    lax.fori_loop(0, pair_count, pair, 0)


def route_kernel(
    shot, pairs, owners, own, outgoing, filled, left, right, rates,
    *, patches, pair_count, shot_count, inverse,
):
    rows_own = 2 * (patches + pair_count)
    outgoing[...] = jnp.zeros_like(outgoing)
    for o in range(shot_count):
        filled[o] = 0
    first = 2 * shot[0]
    lane = iota((patches, PB), 1)
    counts = own[rows_own : rows_own + patches, :]
    for r in range(2):
        mine = jnp.sum(jnp.where(lane == first + r, counts, 0.0), axis=1, keepdims=True)
        rates[pl.ds(r * patches, patches), :] = jnp.broadcast_to(mine, (patches, PB))
    for k in range(pair_count):
        low, high = ordered(pairs, k)
        cols = own[pl.ds(rows_own + high, 1), :]
        for r in range(2):
            left[2 * k + r : 2 * k + r + 1, :] = rates[pl.ds(r * patches + low, 1), :]
            right[2 * k + r : 2 * k + r + 1, :] = cols
    rates[...] = fit(own[pl.ds(2 * patches, 2 * pair_count), :], left[...], right[...], inverse)

    def entry(k, carry):
        for m in range(2):
            owner = owners[m, k]
            slot = filled[owner]
            filled[owner] = slot + 1
            for r in range(2):
                outgoing[pl.ds(4 * owner + 2 * slot + r, 1), :] = rates[pl.ds(2 * k + r, 1), :]
        return carry

    lax.fori_loop(0, pair_count, entry, 0)


def intra_kernel(shot, panel, own, rates, loads, cumulant, *, patches, rows_own, inverse):
    vectors = own[rows_own:, :]
    first = 2 * shot[0]
    lines = 2 * patches
    lane = iota((lines, PB), 1)
    line = iota((lines, PB), 0)
    cols = jnp.concatenate([vectors[n // 2 : n // 2 + 1, :] for n in range(lines)], axis=0)
    mine = jnp.sum(jnp.where(lane == first + line % 2, cols, 0.0), axis=1, keepdims=True)
    rate = fit(own[:lines, :], mine, cols, inverse)
    rates[...] = rate
    here = lane == (line % 2) * (PB // 2) + panel[0] * patches + line // 2
    sums = jnp.sum(rate, axis=1, keepdims=True)
    loads[...] = jnp.sum(jnp.where(here, sums, 0.0), axis=0, keepdims=True)
    halves = cumulant.shape[1] // PB
    for h in range(halves):
        ij, il, jl, ijl, i, j, l = (
            vectors[patches + m * halves + h : patches + m * halves + h + 1, :] * inverse for m in range(7)
        )
        kappa = ijl - ij * l - il * j - jl * i + 2.0 * i * j * l
        cumulant[:, h * PB : (h + 1) * PB] = 1000.0 * kappa


def owner_kernel(shot, pairs, owners, arrived, boundary, *, shot_count):
    me = shot[0]
    turns = [jnp.int32(0), jnp.int32(0)]
    held = jnp.int32(0)
    for k in range(pairs.shape[1]):
        turn = (pairs[0, k] > pairs[1, k]).astype(jnp.int32)
        for m in range(2):
            hit = owners[m, k] == me
            turns = [jnp.where(hit & (held == slot), turn, t) for slot, t in enumerate(turns)]
            held = held + hit.astype(jnp.int32)
    for slot in range(2):
        span = pl.ds(slot * PB, PB)
        for r in range(2):
            boundary[pl.ds(slot * PB + r, shot_count, stride=2), :] = arrived[
                pl.ds(2 * slot + r, shot_count, stride=4), :
            ]

        @pl.when(turns[slot] == 1)
        def _():
            boundary[span, :] = boundary[span, :].T


def smem():
    return pl.BlockSpec(memory_space=pltpu.SMEM)


def vmem():
    return pl.BlockSpec(memory_space=pltpu.VMEM)


def f32(*shape):
    return jax.ShapeDtypeStruct(shape, jnp.float32)


def near_f32(*shape):
    return pltpu.VMEM(shape, jnp.float32)


def exchange(x, axis):
    return lax.all_to_all(x, axis, split_axis=0, concat_axis=0, tiled=True)


def local(events, pair_patches, pair_owners, triples, *, interpret=False):
    shot_dev, det_dev = events.shape
    shot_count = lax.axis_size(SHOT)
    det_count = lax.axis_size("det")
    shot = lax.axis_index(SHOT).astype(jnp.int32).reshape(1)
    panel = lax.axis_index("det").astype(jnp.int32).reshape(1)
    core = lax.axis_index(SHOT[2]).astype(jnp.int32).reshape(1)
    inverse = 1.0 / float(shot_dev * shot_count)
    patches = det_dev // PB
    near = lax.axis_size(SHOT[0])
    far = lax.axis_size(SHOT[1])
    pairs = pair_patches[0].T
    pair_count = pairs.shape[1]
    owners = pair_owners[0].T
    triple_rows = triples.transpose(2, 0, 1)
    triple_count = triple_rows.shape[2]
    rows_own = 2 * (patches + pair_count)
    vector_rows = 24
    part = far * rows_own + vector_rows
    own_rows = rows_own + vector_rows
    chunks = 4

    keep, send = pl.pallas_call(
        functools.partial(
            count_kernel,
            chunks=chunks,
            patches=patches,
            pair_count=pair_count,
            near=near,
            far=far,
            rows_own=rows_own,
            vector_rows=vector_rows,
        ),
        out_shape=(near_f32(near * part, PB), near_f32(near * part, PB)),
        in_specs=[smem(), smem(), vmem(), pl.BlockSpec(memory_space=pl.ANY)],
        out_specs=(vmem(), vmem()),
        scratch_shapes=[
            pltpu.VMEM((shot_dev, det_dev), jnp.int32),
            pltpu.VMEM((shot_dev, det_dev), jnp.bfloat16),
            pltpu.VMEM((det_dev, shot_dev), jnp.bfloat16),
            pltpu.VMEM((patches * det_dev, PB), jnp.float32),
            pltpu.VMEM((det_dev, 3 * triple_count), jnp.bfloat16),
            pltpu.SemaphoreType.DMA((chunks,)),
        ],
        interpret=interpret,
        name="count",
    )(core, pairs, triple_rows, events)
    other = lax.ppermute(send, SHOT[2], [(0, 1), (1, 0)])
    half = keep + other
    arrived = exchange(half.reshape(near, part, PB), SHOT[0])
    total = arrived.sum(axis=0)
    grams = total[: far * rows_own].reshape(far, rows_own // 4, 4, PB)
    vector = total[far * rows_own :].reshape(1, vector_rows // 4, 4, PB)
    vector = jnp.broadcast_to(vector, (far, *vector.shape[1:]))
    vector = jnp.pad(vector, ((0, 0), (0, (-own_rows % 8) // 4), (0, 0), (0, 0)))
    arrived = exchange(jnp.concatenate([grams, vector], axis=1), SHOT[1])
    own = pltpu.with_memory_space_constraint(arrived.sum(axis=0).reshape(-1, PB), pltpu.VMEM)
    outgoing = pl.pallas_call(
        functools.partial(
            route_kernel,
            patches=patches,
            pair_count=pair_count,
            shot_count=shot_count,
            inverse=inverse,
        ),
        out_shape=near_f32(shot_count * 4, PB),
        in_specs=[smem(), smem(), smem(), vmem()],
        out_specs=vmem(),
        scratch_shapes=[
            pltpu.SMEM((shot_count,), jnp.int32),
            pltpu.VMEM((2 * pair_count, PB), jnp.float32),
            pltpu.VMEM((2 * pair_count, PB), jnp.float32),
            pltpu.VMEM((2 * pair_count, PB), jnp.float32),
        ],
        interpret=interpret,
        name="route",
    )(shot, pairs, owners, own)
    incoming = exchange(outgoing.reshape(shot_count, 4, PB), SHOT)
    rates, loads, cumulant = pl.pallas_call(
        functools.partial(intra_kernel, patches=patches, rows_own=rows_own, inverse=inverse),
        out_shape=(f32(2 * patches, PB), near_f32(1, PB), f32(1, triple_count)),
        in_specs=[smem(), smem(), vmem()],
        out_specs=(vmem(), vmem(), vmem()),
        interpret=interpret,
        name="intra",
    )(shot, panel, own)
    load = lax.all_gather(loads, "det").sum(axis=0)
    detector_load = load.reshape(2, det_count * patches).T
    incoming = pltpu.with_memory_space_constraint(incoming.reshape(4 * shot_count, PB), pltpu.VMEM)
    boundary = pl.pallas_call(
        functools.partial(owner_kernel, shot_count=shot_count),
        out_shape=f32(2 * PB, PB),
        in_specs=[smem(), smem(), smem(), vmem()],
        out_specs=vmem(),
        interpret=interpret,
        name="owner",
    )(shot, pairs, owners, incoming)
    return (
        rates.reshape(patches, 2, PB),
        boundary.reshape(1, 1, 2, PB, PB),
        detector_load,
        cumulant,
    )


def solution(mesh):
    torus = Mesh(
        mesh.devices.reshape(4, 8, 2, mesh.shape["det"]), ("shot_0", "shot_1", "shot_2", "det")
    )
    return jax.shard_map(
        local,
        mesh=torus,
        in_specs=(P(SHOT, "det"), P("det", None, None), P("det", None, None), P("det", None, None)),
        out_specs=(
            P("det", SHOT, None),
            P("det", SHOT, None, None, None),
            P(None, SHOT),
            P("det", None),
        ),
        check_vma=False,
    )
```

time: 156 us -> 87.2 us (0.56); the launches traced: 153 us -> 86.8 us
  local copies, waits for them, and re-layouts: 42.5 us -> 0.68 us
  starting transfers between devices: 31 us -> 11.8 us
  Pallas kernels: 0 us -> 11.1 us
  other arithmetic: 11.5 us -> 1.1 us
  matrix products: 8.11 us -> 0 us
  waiting for transfers between devices: 13.2 us -> 17.1 us
    psum x3 -> x0, blocking collectives: 45.7 us -> none  [by_axis(): x = lax.psum(x, axis)]
    gather x10 -> x0, local copies, waits for them, and re-layouts: 27.1 us -> none  [the longest x3 12.6 us: local(): jnp.take(events, triple_index.reshape(-1), axis=1).astype(jnp.float32)]
    all_to_all x0 -> x1, blocking collectives: none -> 23.1 us  [exchange(): return lax.all_to_all(x, axis, split_axis=0, concat_axis=0, tiled=True)]
    all_gather x0 -> x1, blocking collectives: none -> 21.2 us  [local(): load = lax.all_gather(loads, 'det').sum(axis=0)]
    all_to_all x3 -> x2, starting transfers between devices: 31 us -> 9.89 us  [exchange(): return lax.all_to_all(x, axis, split_axis=0, concat_axis=0, tiled=True)]
    pallas_call x0 -> x4, Pallas kernels: none -> 11.1 us  [the longest x1 6.78 us: local(): pl.pallas_call(functools.partial(count_kernel, chunks=chunks, patches=pat...]
    dot_general x2 -> x0, matrix products: 8.11 us -> none  [the longest x1 7.41 us: local(): jnp.einsum('spi,spj->pij', first_columns, second_columns, preferred_eleme...]
    unnamed x11 -> x0, local copies, waits for them, and re-layouts: 6.97 us -> none
  transfers between devices with their start and end apart: 3 -> 3, of which waited for: 2 -> 2; matrix products, arithmetic and copies ran while one was open for 17% -> 1% of each run, Pallas kernels for 0% -> 1%
where the time goes in v1:
time: 87.2 us; the launch traced here: 86.8 us
  blocking collectives  44.3 us (51%)
  waiting for transfers between devices  17.1 us (20%)
  starting transfers between devices  11.8 us (14%)
  Pallas kernels  11.1 us (13%)
  other arithmetic  1.1 us (1%)
    all_to_all x1, blocking collectives, exchange(): return lax.all_to_all(x, axis, split_axis=0, concat_axis=0, tiled=True)  23.1 us
    all_gather x1, blocking collectives, local(): load = lax.all_gather(loads, 'det').sum(axis=0)  21.2 us
    all_to_all x2, waiting for transfers between devices, exchange(): return lax.all_to_all(x, axis, split_axis=0, concat_axis=0, tiled=True)  14.3 us
    all_to_all x2, starting transfers between devices, exchange(): return lax.all_to_all(x, axis, split_axis=0, concat_axis=0, tiled=True)  9.89 us
    pallas_call x1, Pallas kernels, local(): pl.pallas_call(functools.partial(count_kernel, chunks=chunks, patches=pat...  6.78 us
    ppermute x1, waiting for transfers between devices, local(): other = lax.ppermute(send, SHOT[2], [(0, 1), (1, 0)])  2.79 us
    ppermute x1, starting transfers between devices, local(): other = lax.ppermute(send, SHOT[2], [(0, 1), (1, 0)])  1.92 us
    pallas_call x1, Pallas kernels, local(): pl.pallas_call(functools.partial(route_kernel, patches=patches, pair_coun...  1.83 us
  transfers between devices with their start and end apart: 3, of which 2 were waited for; matrix products, arithmetic and copies ran while one was open for 1% of the time, Pallas kernels for 1%

profile of v1, /device:TPU:6, one launch (start us, length us, event | category | flops | bytes accessed | tf_op | source)
XLA Modules:
  0.0 86.8 jit_solution(7244190796806083561)
XLA Ops:
  0.6 6.8 %count.1 = (f32[2272,128]{1,0:T(8,128)S(1)}, f32[2272,128]{1,0:T(8,128)S(1)}) custom-call(s32[1]{0:T(128)} %bitcast.2.core, s32[2,26]{1,0:T(2,128)} %bitcast.28, s32[3,1,256]{2,1,0:T(1,128)} %bitcast.33, s32[1024,1024]{1,0:T(8,128)} %events.1), custom_call_target="tpu_custom_call" | custom-call | tf_op jit(solution)/shard_map/count/pallas_call | solution.py:232
  7.4 1.9 %collective-permute-start = (f32[2272,128]{1,0:T(8,128)S(1)}, f32[2272,128]{1,0:T(8,128)S(1)}, u32[]{:S(2)}, u32[]{:S(2)}) collective-permute-start(f32[2272,128]{1,0:T(8,128)S(1)} %get-tuple-element.10), channel_id=1, source_target_pairs={{0,8},{8,0},{1,9},{9,1},{2,10},{10,2},{3,11},{11,3},{4,12},{12,4},... | collective-permute-start | bytes 3489800 | tf_op jit(solution)/shard_map/ppermute | solution.py:257
  9.4 2.8 %collective-permute-done = f32[2272,128]{1,0:T(8,128)S(1)} collective-permute-done((f32[2272,128]{1,0:T(8,128)S(1)}, f32[2272,128]{1,0:T(8,128)S(1)}, u32[]{:S(2)}, u32[]{:S(2)}) %collective-permute-start) | collective-permute-done | bytes 1163296 | tf_op jit(solution)/shard_map/ppermute | solution.py:257
  12.1 0.1 add.13
  12.3 23.1 %all_to_all.15 = f32[4,568,128]{2,1,0:T(8,128)S(1)} all-to-all(f32[4,568,128]{2,1,0:T(8,128)S(1)} %bitcast.24), channel_id=1, replica_groups=mesh['shot_0'=4,'shot_1'=8,'shot_2'=2,'det'=8] {'shot_0'}, dimensions={0} | all-to-all | bytes 2326528 | tf_op jit(solution)/shard_map/all_to_all | solution.py:207
  35.3 0.1 reduce_sum.27
  35.5 0.8 select_maximum_fusion
  36.3 3.5 %all-to-all-start.1 = ((f32[8,24,4,128]{3,2,1,0:T(4,128)}), f32[8,24,4,128]{3,2,1,0:T(4,128)S(1)}, u32[]{:S(2)}, u32[]{:S(2)}) async-start(f32[8,24,4,128]{3,2,1,0:T(4,128)} %select_maximum_fusion), calls=%async_computation.1 | async-start | bytes 786432 | tf_op jit(solution)/shard_map/all_to_all | solution.py:207
  39.8 14.3 %all-to-all-done.1 = f32[8,24,4,128]{3,2,1,0:T(4,128)S(1)} async-done(((f32[8,24,4,128]{3,2,1,0:T(4,128)}), f32[8,24,4,128]{3,2,1,0:T(4,128)S(1)}, u32[]{:S(2)}, u32[]{:S(2)}) %all-to-all-start.1) | async-done | bytes 393248 | tf_op jit(solution)/shard_map/all_to_all | solution.py:207
  54.1 0.1 reduce_sum.28
  54.1 1.8 %route.1 = f32[256,128]{1,0:T(8,128)} custom-call(s32[1]{0:T(128)} %bitcast.shot, s32[2,26]{1,0:T(2,128)} %bitcast.29, s32[2,26]{1,0:T(2,128)} %bitcast.31, f32[96,128]{1,0:T(8,128)S(1)} %bitcast.21), custom_call_target="tpu_custom_call" | custom-call | tf_op jit(solution)/shard_map/route/pallas_call | solution.py:267
  56.0 6.4 %all-to-all-start.2 = ((f32[64,4,128]{2,1,0:T(4,128)}), f32[64,4,128]{2,1,0:T(4,128)S(1)}, u32[]{:S(2)}, u32[]{:S(2)}) async-start(f32[64,4,128]{2,1,0:T(4,128)} %bitcast.15), calls=%async_computation.2 | async-start | bytes 262144 | tf_op jit(solution)/shard_map/all_to_all | solution.py:207
  62.4 0.7 intra.1
  63.2 21.2 %all-gather.1 = f32[8,1,128]{2,1,0:T(1,128)S(1)} all-gather(f32[1,1,128]{2,1,0:T(1,128)S(1)} %bitcast.23), channel_id=2, replica_groups=mesh['shot_0'=4,'shot_1'=8,'shot_2'=2,'det'=8] {'det'}, dimensions={0}, use_global_device_ids=true | all-gather | bytes 4608 | tf_op jit(solution)/shard_map/all_gather | solution.py:296
  84.4 0.6 reshape.55
  85.1 0.0 all-to-all-done.2
  85.1 1.8 %owner.1 = f32[256,128]{1,0:T(8,128)} custom-call(s32[1]{0:T(128)} %bitcast.shot, s32[2,26]{1,0:T(2,128)} %bitcast.30, s32[2,26]{1,0:T(2,128)} %bitcast.32, f32[256,128]{1,0:T(8,128)S(1)} %bitcast.20), custom_call_target="tpu_custom_call" | custom-call | tf_op jit(solution)/shard_map/owner/pallas_call | solution.py:299
  (4 shorter events, 0.1 us)
Async XLA Ops:
  7.4 4.7 %collective-permute-start = (f32[2272,128]{1,0:T(8,128)S(1)}, f32[2272,128]{1,0:T(8,128)S(1)}, u32[]{:S(2)}, u32[]{:S(2)}) collective-permute-start(f32[2272,128]{1,0:T(8,128)S(1)} %get-tuple-element.10), channel_id=1, source_target_pairs={{0,8},{8,0},{1,9},{9,1},{2,10},{10,2},{3,11},{11,3},{4,12},{12,4},... | collective-permute-start | bytes 3489800 | tf_op jit(solution)/shard_map/ppermute | solution.py:257
  36.3 17.8 %all-to-all-start.1 = ((f32[8,24,4,128]{3,2,1,0:T(4,128)}), f32[8,24,4,128]{3,2,1,0:T(4,128)S(1)}, u32[]{:S(2)}, u32[]{:S(2)}) async-start(f32[8,24,4,128]{3,2,1,0:T(4,128)} %select_maximum_fusion), calls=%async_computation.1 | async-start | bytes 786432 | tf_op jit(solution)/shard_map/all_to_all | solution.py:207
  56.0 29.1 %all-to-all-start.2 = ((f32[64,4,128]{2,1,0:T(4,128)}), f32[64,4,128]{2,1,0:T(4,128)S(1)}, u32[]{:S(2)}, u32[]{:S(2)}) async-start(f32[64,4,128]{2,1,0:T(4,128)} %bitcast.15), calls=%async_computation.2 | async-start | bytes 262144 | tf_op jit(solution)/shard_map/all_to_all | solution.py:207

commit v2 on v1

v2 whole, which is shorter than its diff:
```python
import functools

import jax
import jax.numpy as jnp
from jax import lax
from jax.experimental import pallas as pl
from jax.experimental.pallas import tpu as pltpu
from jax.sharding import Mesh
from jax.sharding import PartitionSpec as P

PB = 128
SHOT = ("shot_0", "shot_1", "shot_2")
SLOT_ROWS = 8


def fit(joint, rows, cols, inverse):
    u = joint * inverse
    x = rows * inverse
    y = cols * inverse
    den = jnp.maximum(1.0 - 2.0 * x - 2.0 * y + 4.0 * u, 0.25)
    q = (u - x * y) / den
    return 100.0 * (0.5 - 0.5 * jnp.sqrt(jnp.maximum(1.0 - 4.0 * q, 0.04)))


def iota(shape, dim):
    return lax.broadcasted_iota(jnp.int32, shape, dim)


def ordered(pairs, k):
    return jnp.minimum(pairs[0, k], pairs[1, k]), jnp.maximum(pairs[0, k], pairs[1, k])


def table_kernel(shot, panel, pairs, owners, table, filled, *, shot_count):
    table[6, 0] = shot[0]
    table[6, 1] = panel[0]

    def clear(o, carry):
        filled[o] = 0
        return carry

    lax.fori_loop(0, shot_count, clear, 0)

    def pair(k, carry):
        for m in range(2):
            owner = owners[m, k]
            slot = filled[owner]
            filled[owner] = slot + 1
            table[m, k] = owner * SLOT_ROWS + 2 * slot
            table[2 + m, k] = owner * SLOT_ROWS + 5 + slot
        low, high = ordered(pairs, k)
        table[4, k] = low
        table[5, k] = high
        table[7, k] = (pairs[0, k] > pairs[1, k]).astype(jnp.int32)
        return carry

    lax.fori_loop(0, pairs.shape[1], pair, 0)


def count_kernel(
    shot_in, pairs_in, triples_in, events, keep, send,
    raw, bits, flipped, grams, picker, shot, pairs, triple_rows, small, sems,
    *, chunks, patches, pair_count, near, far, rows_own,
):
    shots, dets = raw.shape
    step = shots // chunks
    triple_count = triple_rows.shape[2]
    copies = [
        pltpu.make_async_copy(events.at[pl.ds(i * step, step)], raw.at[pl.ds(i * step, step)], sems.at[i])
        for i in range(chunks)
    ]
    few = [
        pltpu.make_async_copy(source, target, small.at[i])
        for i, (source, target) in enumerate(((triples_in, triple_rows), (pairs_in, pairs), (shot_in, shot)))
    ]
    few[0].start()
    for copy in (*copies, *few[1:]):
        copy.start()
    few[0].wait()
    detector = iota((dets, triple_count), 0)
    for m in range(3):
        hit = detector == triple_rows[m]
        picker[:, m * triple_count : (m + 1) * triple_count] = jnp.where(hit, 1.0, 0.0).astype(jnp.float8_e4m3fn)
    counts = jnp.zeros((1, dets), jnp.float32)
    sums = [jnp.zeros((1, triple_count), jnp.float32) for _ in range(7)]
    wide = 2 * PB

    def add_grams(first, last, fresh):
        for j in range(dets // wide):
            height = (j + 1) * wide
            panel = jnp.dot(
                flipped[:height, first:last],
                bits[first:last, j * wide : (j + 1) * wide],
                preferred_element_type=jnp.float32,
            )
            for h in range(2):
                span = slice((2 * j + h) * dets, (2 * j + h) * dets + height)
                part = panel[:, h * PB : (h + 1) * PB]
                grams[span, :] = part if fresh else grams[span, :] + part

    for i in range(chunks):
        copies[i].wait()
        span = slice(i * step, (i + 1) * step)
        values = raw[span, :].astype(jnp.float32)
        counts += jnp.sum(values, axis=0, keepdims=True)
        narrow = values.astype(jnp.bfloat16)
        bits[span, :] = narrow
        flipped[:, span] = narrow.T
        picked = jnp.dot(values.astype(jnp.float8_e4m3fn), picker[...], preferred_element_type=jnp.float32)
        a, b, c = (picked[:, m * triple_count : (m + 1) * triple_count] for m in range(3))
        ab = a * b
        terms = (ab, a * c, b * c, ab * c, a, b, c)
        sums = [s + jnp.sum(t, axis=0, keepdims=True) for s, t in zip(sums, terms, strict=True)]
        if i == chunks // 2 - 1:
            add_grams(0, shots // 2, True)
    add_grams(shots // 2, shots, False)
    part = far * rows_own + patches
    group = triple_count // far
    zeros = jnp.zeros((far, PB), jnp.float32)
    lines = []
    for n in range(0, len(sums), PB // group):
        members = sums[n : n + PB // group]
        members += [jnp.zeros((1, triple_count), jnp.float32)] * (PB // group - len(members))
        rows = [
            jnp.concatenate([t[:, y * group : (y + 1) * group] for t in members], axis=1) for y in range(far)
        ]
        lines.append(jnp.concatenate(rows, axis=0))
    lines += [zeros] * (rows_own - 2 * (patches + pair_count) - len(lines))
    for target in (keep, send):
        for x in range(near):
            for n, line in enumerate(lines):
                row = x * part + 2 * (patches + pair_count) + n
                target[pl.ds(row, far, stride=rows_own), :] = line
            for p in range(patches):
                row = (x + 1) * part - patches + p
                target[row : row + 1, :] = counts[:, p * PB : (p + 1) * PB]
    few[1].wait()
    few[2].wait()
    mine = shot[0] % 2

    def place(block, start):
        for target, side in ((keep, mine), (send, 1 - mine)):
            for x in range(near):
                for r in range(2):
                    rows = grams[pl.ds(start + 4 * far * x + 2 * side + r, far, stride=4), :]
                    target[pl.ds(x * part + 2 * block + r, far, stride=rows_own), :] = rows

    for p in range(patches):
        place(p, p * dets + p * PB)

    def pair(k, carry):
        low, high = ordered(pairs, k)
        place(patches + k, high * dets + low * PB)
        return carry

    lax.fori_loop(0, pair_count, pair, 0)


def fold_kernel(arrived, payload, *, near, far, rows_own, patches):
    part = far * rows_own + patches

    def total(start, rows):
        value = arrived[start : start + rows, :]
        for x in range(1, near):
            value += arrived[x * part + start : x * part + start + rows, :]
        return value

    counts = total(far * rows_own, patches)
    for y in range(far):
        row = y * (rows_own + patches)
        payload[row : row + rows_own, :] = total(y * rows_own, rows_own)
        payload[row + rows_own : row + rows_own + patches, :] = counts


def route_kernel(
    table, arrived, outgoing, intra, loads, own, left, right, rates,
    *, patches, pair_count, far, group, inverse,
):
    total = arrived[0]
    for y in range(1, far):
        total += arrived[y]
    own[...] = total
    vector_row = 2 * (patches + pair_count)
    counts_row = total.shape[0] - patches
    first = 2 * table[6, 0]
    lines = 2 * patches
    lane = iota((lines, PB), 1)
    line = iota((lines, PB), 0)
    counts = own[counts_row:, :]
    both = jnp.concatenate([counts, counts], axis=0)
    mine = jnp.sum(jnp.where(lane == first + line // patches, both, 0.0), axis=1, keepdims=True)
    rates[:lines, :] = jnp.broadcast_to(mine, (lines, PB))
    for k in range(pair_count):
        low, high = table[4, k], table[5, k]
        cols = own[pl.ds(counts_row + high, 1), :]
        for r in range(2):
            left[2 * k + r : 2 * k + r + 1, :] = rates[pl.ds(r * patches + low, 1), :]
            right[2 * k + r : 2 * k + r + 1, :] = cols
    rates[...] = fit(own[lines : lines + 2 * pair_count, :], left[...], right[...], inverse)
    terms = []
    for n in range(7):
        row = vector_row + n * group // PB
        at = n * group % PB
        terms.append(own[row : row + 1, at : at + group] * inverse)
    ij, il, jl, ijl, i, j, l = terms
    kappa = ijl - ij * l - il * j - jl * i + 2.0 * i * j * l
    kappa = jnp.concatenate([1000.0 * kappa, jnp.zeros((1, PB - group), jnp.float32)], axis=1)
    base = jnp.where(iota((SLOT_ROWS, PB), 0) == 4, kappa, 0.0)
    for o in range(outgoing.shape[0] // SLOT_ROWS):
        outgoing[o * SLOT_ROWS : (o + 1) * SLOT_ROWS, :] = base
    for k in range(pair_count):
        turned = jnp.full((1, PB), table[7, k].astype(jnp.float32), jnp.float32)
        for m in range(2):
            at = table[m, k]
            outgoing[pl.ds(table[2 + m, k], 1), :] = turned
            for r in range(2):
                outgoing[pl.ds(at + r, 1), :] = rates[2 * k + r : 2 * k + r + 1, :]
    cols = jnp.concatenate([counts[n // 2 : n // 2 + 1, :] for n in range(lines)], axis=0)
    mine = jnp.sum(jnp.where(lane == first + line % 2, cols, 0.0), axis=1, keepdims=True)
    rate = fit(own[:lines, :], mine, cols, inverse)
    intra[...] = rate
    here = lane == (line % 2) * (PB // 2) + table[6, 1] * patches + line // 2
    sums = jnp.sum(rate, axis=1, keepdims=True)
    loads[...] = jnp.sum(jnp.where(here, sums, 0.0), axis=0, keepdims=True)


def owner_kernel(panels, arrived, boundary, loads, cumulant, *, shot_count, far, group):
    for slot in range(2):
        span = pl.ds(slot * PB, PB)
        for r in range(2):
            boundary[pl.ds(slot * PB + r, shot_count, stride=2), :] = arrived[
                pl.ds(2 * slot + r, shot_count, stride=SLOT_ROWS), :
            ]
        straight = boundary[span, :]
        turned = arrived[5 + slot : 6 + slot, :] > 0.5
        boundary[span, :] = jnp.where(turned, straight.T, straight)
    load = jnp.sum(panels[...], axis=0, keepdims=True)
    half = PB // 2
    loads[...] = jnp.concatenate([load[:, :half], load[:, half:]], axis=0)
    for y in range(far):
        row = 2 * y * SLOT_ROWS + 4
        cumulant[:, y * group : (y + 1) * group] = arrived[row : row + 1, :group]


def smem():
    return pl.BlockSpec(memory_space=pltpu.SMEM)


def vmem():
    return pl.BlockSpec(memory_space=pltpu.VMEM)


def f32(*shape):
    return jax.ShapeDtypeStruct(shape, jnp.float32)


def near_f32(*shape):
    return pltpu.VMEM(shape, jnp.float32)


def within(x):
    return pltpu.with_memory_space_constraint(x, pltpu.VMEM)


def exchange(x, axis):
    return lax.all_to_all(x, axis, split_axis=0, concat_axis=0, tiled=True)


def local(events, pair_patches, pair_owners, triples, *, interpret=False):
    shot_dev, det_dev = events.shape
    shot_count = lax.axis_size(SHOT)
    det_count = lax.axis_size("det")
    shot = lax.axis_index(SHOT).astype(jnp.int32).reshape(1)
    panel = lax.axis_index("det").astype(jnp.int32).reshape(1)
    inverse = 1.0 / float(shot_dev * shot_count)
    patches = det_dev // PB
    near = lax.axis_size(SHOT[0])
    far = lax.axis_size(SHOT[1])
    pairs = pair_patches[0].T
    pair_count = pairs.shape[1]
    owners = pair_owners[0].T
    triple_rows = triples.transpose(2, 0, 1)
    triple_count = triple_rows.shape[2]
    group = triple_count // far
    rows_own = 2 * (patches + pair_count) + 4
    own_rows = rows_own + patches
    part = far * rows_own + patches
    chunks = 4

    keep, send = pl.pallas_call(
        functools.partial(
            count_kernel,
            chunks=chunks,
            patches=patches,
            pair_count=pair_count,
            near=near,
            far=far,
            rows_own=rows_own,
        ),
        out_shape=(near_f32(near * part, PB), near_f32(near * part, PB)),
        in_specs=[pl.BlockSpec(memory_space=pl.ANY)] * 4,
        out_specs=(vmem(), vmem()),
        scratch_shapes=[
            pltpu.VMEM((shot_dev, det_dev), jnp.int32),
            pltpu.VMEM((shot_dev, det_dev), jnp.bfloat16),
            pltpu.VMEM((det_dev, shot_dev), jnp.bfloat16),
            pltpu.VMEM((patches * det_dev, PB), jnp.float32),
            pltpu.VMEM((det_dev, 3 * triple_count), jnp.float8_e4m3fn),
            pltpu.SMEM((1,), jnp.int32),
            pltpu.SMEM((2, pair_count), jnp.int32),
            pltpu.VMEM((3, 1, triple_count), jnp.int32),
            pltpu.SemaphoreType.DMA((3,)),
            pltpu.SemaphoreType.DMA((chunks,)),
        ],
        interpret=interpret,
        name="count",
    )(shot, pairs, triple_rows, events)
    late_pairs, late_owners, _ = lax.optimization_barrier((pairs, owners, send))
    table = pl.pallas_call(
        functools.partial(table_kernel, shot_count=shot_count),
        out_shape=jax.ShapeDtypeStruct((8, pair_count), jnp.int32),
        in_specs=[smem()] * 4,
        out_specs=smem(),
        scratch_shapes=[pltpu.SMEM((shot_count,), jnp.int32)],
        interpret=interpret,
        name="table",
    )(shot, panel, late_pairs, late_owners)
    other = lax.ppermute(send, SHOT[2], [(0, 1), (1, 0)])
    half = keep + other
    arrived = exchange(half.reshape(near, part, PB), SHOT[0])
    payload = pl.pallas_call(
        functools.partial(fold_kernel, near=near, far=far, rows_own=rows_own, patches=patches),
        out_shape=near_f32(far * own_rows, PB),
        in_specs=[vmem()],
        out_specs=vmem(),
        interpret=interpret,
        name="fold",
    )(within(arrived.reshape(near * part, PB)))
    arrived = exchange(payload.reshape(far, own_rows, PB), SHOT[1])
    outgoing, rates, loads = pl.pallas_call(
        functools.partial(
            route_kernel, patches=patches, pair_count=pair_count, far=far, group=group, inverse=inverse
        ),
        out_shape=(near_f32(shot_count * SLOT_ROWS, PB), f32(2 * patches, PB), near_f32(1, PB)),
        in_specs=[smem(), vmem()],
        out_specs=(vmem(), vmem(), vmem()),
        scratch_shapes=[
            pltpu.VMEM((own_rows, PB), jnp.float32),
            pltpu.VMEM((2 * pair_count, PB), jnp.float32),
            pltpu.VMEM((2 * pair_count, PB), jnp.float32),
            pltpu.VMEM((2 * pair_count, PB), jnp.float32),
        ],
        interpret=interpret,
        name="route",
    )(table, within(arrived))
    incoming = exchange(outgoing.reshape(shot_count, SLOT_ROWS, PB), SHOT)
    panels = lax.all_gather(loads, "det").reshape(det_count, PB)
    boundary, load, cumulant = pl.pallas_call(
        functools.partial(owner_kernel, shot_count=shot_count, far=far, group=group),
        out_shape=(f32(2 * PB, PB), f32(2, det_count * patches), f32(1, triple_count)),
        in_specs=[vmem(), vmem()],
        out_specs=(vmem(), vmem(), vmem()),
        interpret=interpret,
        name="owner",
    )(within(panels), within(incoming.reshape(SLOT_ROWS * shot_count, PB)))
    return (
        rates.reshape(patches, 2, PB),
        boundary.reshape(1, 1, 2, PB, PB),
        load.T,
        cumulant,
    )


def solution(mesh):
    torus = Mesh(
        mesh.devices.reshape(4, 8, 2, mesh.shape["det"]), ("shot_0", "shot_1", "shot_2", "det")
    )
    return jax.shard_map(
        local,
        mesh=torus,
        in_specs=(P(SHOT, "det"), P("det", None, None), P("det", None, None), P("det", None, None)),
        out_specs=(
            P("det", SHOT, None),
            P("det", SHOT, None, None, None),
            P(None, SHOT),
            P("det", None),
        ),
        check_vma=False,
    )
```

time: 87.2 us -> 82.8 us (0.950)
  waiting for transfers between devices: 17.1 us -> 13.6 us
  other arithmetic: 1.1 us -> 0.12 us
    all_to_all x2, waiting for transfers between devices: 14.3 us -> 10.7 us  [exchange(): return lax.all_to_all(x, axis, split_axis=0, concat_axis=0, tiled=True)]
    pallas_call x2 -> x3, Pallas kernels: 2.47 us -> 3.74 us  [the longest x1 2.17 us: local(): pl.pallas_call(functools.partial(table_kernel, shot_count=shot_count), ou...]
    pallas_call x1, Pallas kernels: 6.78 us -> 5.76 us  [local(): pl.pallas_call(functools.partial(count_kernel, chunks=chunks, patches=pat...]
  transfers between devices with their start and end apart: 3 -> 3, of which waited for: 2 -> 2; matrix products, arithmetic and copies ran while one was open for 1% -> 0% of each run, Pallas kernels for 1% -> 3%
where the time goes in v2:
time: 82.8 us; the launch traced here: 82.4 us
  blocking collectives  45 us (54%)
  waiting for transfers between devices  13.6 us (16%)
  starting transfers between devices  11.8 us (14%)
  Pallas kernels  11.2 us (14%)
    all_to_all x1, blocking collectives, exchange(): return lax.all_to_all(x, axis, split_axis=0, concat_axis=0, tiled=True)  23.4 us
    all_gather x1, blocking collectives, local(): panels = lax.all_gather(loads, 'det').reshape(det_count, PB)  21.6 us
    all_to_all x2, waiting for transfers between devices, exchange(): return lax.all_to_all(x, axis, split_axis=0, concat_axis=0, tiled=True)  10.7 us
    all_to_all x2, starting transfers between devices, exchange(): return lax.all_to_all(x, axis, split_axis=0, concat_axis=0, tiled=True)  9.86 us
    pallas_call x1, Pallas kernels, local(): pl.pallas_call(functools.partial(count_kernel, chunks=chunks, patches=pat...  5.76 us
    ppermute x1, waiting for transfers between devices, local(): other = lax.ppermute(send, SHOT[2], [(0, 1), (1, 0)])  2.84 us
    pallas_call x1, Pallas kernels, local(): pl.pallas_call(functools.partial(table_kernel, shot_count=shot_count), ou...  2.17 us
    ppermute x1, starting transfers between devices, local(): other = lax.ppermute(send, SHOT[2], [(0, 1), (1, 0)])  1.92 us
  transfers between devices with their start and end apart: 3, of which 2 were waited for; matrix products, arithmetic and copies ran while one was open for 0% of the time, Pallas kernels for 3%

profile of v2, /device:TPU:6, one launch (start us, length us, event | category | flops | bytes accessed | tf_op | source)
XLA Modules:
  0.0 82.4 jit_solution(18421329608424077939)
XLA Ops:
  0.6 5.8 %count.1 = (f32[2336,128]{1,0:T(8,128)S(1)}, f32[2336,128]{1,0:T(8,128)S(1)}) custom-call(s32[1]{0:T(128)} %bitcast.shot_in.shot, s32[2,26]{1,0:T(2,128)} %bitcast.24, s32[3,1,256]{2,1,0:T(1,128)} %bitcast.26, s32[1024,1024]{1,0:T(8,128)} %events.1), custom_call_target="tpu_custom_call" | custom-call | tf_op jit(solution)/shard_map/count/pallas_call | solution.py:289
  6.4 1.9 %collective-permute-start = (f32[2336,128]{1,0:T(8,128)S(1)}, f32[2336,128]{1,0:T(8,128)S(1)}, u32[]{:S(2)}, u32[]{:S(2)}) collective-permute-start(f32[2336,128]{1,0:T(8,128)S(1)} %get-tuple-element.14), channel_id=1, source_target_pairs={{0,8},{8,0},{1,9},{9,1},{2,10},{10,2},{3,11},{11,3},{4,12},{12,4},... | collective-permute-start | bytes 3588104 | tf_op jit(solution)/shard_map/ppermute | solution.py:327
  8.3 2.8 %collective-permute-done = f32[2336,128]{1,0:T(8,128)S(1)} collective-permute-done((f32[2336,128]{1,0:T(8,128)S(1)}, f32[2336,128]{1,0:T(8,128)S(1)}, u32[]{:S(2)}, u32[]{:S(2)}) %collective-permute-start) | collective-permute-done | bytes 1196064 | tf_op jit(solution)/shard_map/ppermute | solution.py:327
  11.2 0.1 add.11
  11.3 23.4 %all_to_all.15 = f32[4,584,128]{2,1,0:T(8,128)S(1)} all-to-all(f32[4,584,128]{2,1,0:T(8,128)S(1)} %bitcast.23), channel_id=1, replica_groups=mesh['shot_0'=4,'shot_1'=8,'shot_2'=2,'det'=8] {'shot_0'}, dimensions={0} | all-to-all | bytes 2392064 | tf_op jit(solution)/shard_map/all_to_all | solution.py:265
  34.7 0.8 fold.1
  35.5 3.4 %all-to-all-start.1 = ((f32[8,80,128]{2,1,0:T(8,128)}), f32[8,80,128]{2,1,0:T(8,128)S(1)}, u32[]{:S(2)}, u32[]{:S(2)}) async-start(f32[8,80,128]{2,1,0:T(8,128)} %bitcast.10), calls=%async_computation.1 | async-start | bytes 655360 | tf_op jit(solution)/shard_map/all_to_all | solution.py:265
  38.9 2.2 %table.1 = s32[8,26]{1,0:T(8,128)} custom-call(s32[1]{0:T(128)} %bitcast.shot_in.shot, s32[1]{0:T(128)} %bitcast.1.panel, s32[2,26]{1,0:T(2,128)} %bitcast.25, s32[2,26]{1,0:T(2,128)} %bitcast.27), custom_call_target="tpu_custom_call" | custom-call | tf_op jit(solution)/shard_map/table/pallas_call | solution.py:318
  41.1 10.7 %all-to-all-done.1.arrived = f32[8,80,128]{2,1,0:T(8,128)S(1)} async-done(((f32[8,80,128]{2,1,0:T(8,128)}), f32[8,80,128]{2,1,0:T(8,128)S(1)}, u32[]{:S(2)}, u32[]{:S(2)}) %all-to-all-start.1) | async-done | bytes 327712 | tf_op jit(solution)/shard_map/all_to_all | solution.py:265
  51.8 1.7 %route.1 = (f32[512,128]{1,0:T(8,128)}, f32[16,128]{1,0:T(8,128)}, f32[1,128]{1,0:T(1,128)S(1)}) custom-call(s32[8,26]{1,0:T(8,128)} %table.1, f32[8,80,128]{2,1,0:T(8,128)S(1)} %all-to-all-done.1.arrived), custom_call_target="tpu_custom_call" | custom-call | tf_op jit(solution)/shard_map/route/pallas_call | solution.py:339
  53.6 6.4 %all-to-all-start.2 = ((f32[64,8,128]{2,1,0:T(8,128)}), f32[64,8,128]{2,1,0:T(8,128)S(1)}, u32[]{:S(2)}, u32[]{:S(2)}) async-start(f32[64,8,128]{2,1,0:T(8,128)} %bitcast.14), calls=%async_computation.2 | async-start | bytes 524288 | tf_op jit(solution)/shard_map/all_to_all | solution.py:265
  60.0 21.6 %all-gather.1 = f32[8,1,128]{2,1,0:T(1,128)S(1)} all-gather(f32[1,1,128]{2,1,0:T(1,128)S(1)} %bitcast.22), channel_id=2, replica_groups=mesh['shot_0'=4,'shot_1'=8,'shot_2'=2,'det'=8] {'det'}, dimensions={0}, use_global_device_ids=true | all-gather | bytes 4608 | tf_op jit(solution)/shard_map/all_gather | solution.py:356
  81.6 0.0 all-to-all-done.2
  81.6 0.8 owner.1
Async XLA Ops:
  6.4 4.8 %collective-permute-start = (f32[2336,128]{1,0:T(8,128)S(1)}, f32[2336,128]{1,0:T(8,128)S(1)}, u32[]{:S(2)}, u32[]{:S(2)}) collective-permute-start(f32[2336,128]{1,0:T(8,128)S(1)} %get-tuple-element.14), channel_id=1, source_target_pairs={{0,8},{8,0},{1,9},{9,1},{2,10},{10,2},{3,11},{11,3},{4,12},{12,4},... | collective-permute-start | bytes 3588104 | tf_op jit(solution)/shard_map/ppermute | solution.py:327
  35.5 16.4 %all-to-all-start.1 = ((f32[8,80,128]{2,1,0:T(8,128)}), f32[8,80,128]{2,1,0:T(8,128)S(1)}, u32[]{:S(2)}, u32[]{:S(2)}) async-start(f32[8,80,128]{2,1,0:T(8,128)} %bitcast.10), calls=%async_computation.1 | async-start | bytes 655360 | tf_op jit(solution)/shard_map/all_to_all | solution.py:265
  53.6 28.0 %all-to-all-start.2 = ((f32[64,8,128]{2,1,0:T(8,128)}), f32[64,8,128]{2,1,0:T(8,128)S(1)}, u32[]{:S(2)}, u32[]{:S(2)}) async-start(f32[64,8,128]{2,1,0:T(8,128)} %bitcast.14), calls=%async_computation.2 | async-start | bytes 524288 | tf_op jit(solution)/shard_map/all_to_all | solution.py:265

commit v3 on v2

--- a/solution.py
+++ b/solution.py
@@ -30,17 +30,12 @@
     return jnp.minimum(pairs[0, k], pairs[1, k]), jnp.maximum(pairs[0, k], pairs[1, k])
 
 
-def table_kernel(shot, panel, pairs, owners, table, filled, *, shot_count):
-    table[6, 0] = shot[0]
-    table[6, 1] = panel[0]
-
-    def clear(o, carry):
+def fill_table(shot, panel, pairs, owners, table, filled):
+    for n in range(pairs.shape[1]):
+        table[6, n] = shot[0] if n == 0 else panel[0]
+    for o in range(filled.shape[0]):
         filled[o] = 0
-        return carry
-
-    lax.fori_loop(0, shot_count, clear, 0)
-
-    def pair(k, carry):
+    for k in range(pairs.shape[1]):
         for m in range(2):
             owner = owners[m, k]
             slot = filled[owner]
@@ -51,14 +46,11 @@
         table[4, k] = low
         table[5, k] = high
         table[7, k] = (pairs[0, k] > pairs[1, k]).astype(jnp.int32)
-        return carry
-
-    lax.fori_loop(0, pairs.shape[1], pair, 0)
 
 
 def count_kernel(
-    shot_in, pairs_in, triples_in, events, keep, send,
-    raw, bits, flipped, grams, picker, shot, pairs, triple_rows, small, sems,
+    shot_in, panel_in, pairs_in, owners_in, triples_in, events, keep, send, table_out,
+    raw, bits, flipped, grams, picker, shot, panel, pairs, owners, table, filled, triple_rows, small, sems,
     *, chunks, patches, pair_count, near, far, rows_own,
 ):
     shots, dets = raw.shape
@@ -68,18 +60,25 @@
         pltpu.make_async_copy(events.at[pl.ds(i * step, step)], raw.at[pl.ds(i * step, step)], sems.at[i])
         for i in range(chunks)
     ]
-    few = [
-        pltpu.make_async_copy(source, target, small.at[i])
-        for i, (source, target) in enumerate(((triples_in, triple_rows), (pairs_in, pairs), (shot_in, shot)))
-    ]
-    few[0].start()
-    for copy in (*copies, *few[1:]):
+    given = (
+        (triples_in, triple_rows),
+        (pairs_in, pairs),
+        (owners_in, owners),
+        (shot_in, shot),
+        (panel_in, panel),
+    )
+    few = [pltpu.make_async_copy(source, target, small.at[i]) for i, (source, target) in enumerate(given)]
+    copy_table = pltpu.make_async_copy(table, table_out, small.at[len(few)])
+    for copy in (*few, *copies):
         copy.start()
-    few[0].wait()
+    for copy in few:
+        copy.wait()
+    fill_table(shot, panel, pairs, owners, table, filled)
     detector = iota((dets, triple_count), 0)
     for m in range(3):
         hit = detector == triple_rows[m]
         picker[:, m * triple_count : (m + 1) * triple_count] = jnp.where(hit, 1.0, 0.0).astype(jnp.float8_e4m3fn)
+    copy_table.start()
     counts = jnp.zeros((1, dets), jnp.float32)
     sums = [jnp.zeros((1, triple_count), jnp.float32) for _ in range(7)]
     wide = 2 * PB
@@ -133,8 +132,6 @@
             for p in range(patches):
                 row = (x + 1) * part - patches + p
                 target[row : row + 1, :] = counts[:, p * PB : (p + 1) * PB]
-    few[1].wait()
-    few[2].wait()
     mine = shot[0] % 2
 
     def place(block, start):
@@ -147,12 +144,9 @@
     for p in range(patches):
         place(p, p * dets + p * PB)
 
-    def pair(k, carry):
-        low, high = ordered(pairs, k)
-        place(patches + k, high * dets + low * PB)
-        return carry
-
-    lax.fori_loop(0, pair_count, pair, 0)
+    for k in range(pair_count):
+        place(patches + k, table[5, k] * dets + table[4, k] * PB)
+    copy_table.wait()
 
 
 def fold_kernel(arrived, payload, *, near, far, rows_own, patches):
@@ -286,7 +280,7 @@
     part = far * rows_own + patches
     chunks = 4
 
-    keep, send = pl.pallas_call(
+    keep, send, table = pl.pallas_call(
         functools.partial(
             count_kernel,
             chunks=chunks,
@@ -296,9 +290,13 @@
             far=far,
             rows_own=rows_own,
         ),
-        out_shape=(near_f32(near * part, PB), near_f32(near * part, PB)),
-        in_specs=[pl.BlockSpec(memory_space=pl.ANY)] * 4,
-        out_specs=(vmem(), vmem()),
+        out_shape=(
+            near_f32(near * part, PB),
+            near_f32(near * part, PB),
+            jax.ShapeDtypeStruct((8, pair_count), jnp.int32),
+        ),
+        in_specs=[pl.BlockSpec(memory_space=pl.ANY)] * 6,
+        out_specs=(vmem(), vmem(), pl.BlockSpec(memory_space=pl.ANY)),
         scratch_shapes=[
             pltpu.VMEM((shot_dev, det_dev), jnp.int32),
             pltpu.VMEM((shot_dev, det_dev), jnp.bfloat16),
@@ -306,24 +304,18 @@
             pltpu.VMEM((patches * det_dev, PB), jnp.float32),
             pltpu.VMEM((det_dev, 3 * triple_count), jnp.float8_e4m3fn),
             pltpu.SMEM((1,), jnp.int32),
+            pltpu.SMEM((1,), jnp.int32),
             pltpu.SMEM((2, pair_count), jnp.int32),
+            pltpu.SMEM((2, pair_count), jnp.int32),
+            pltpu.SMEM((8, pair_count), jnp.int32),
+            pltpu.SMEM((shot_count,), jnp.int32),
             pltpu.VMEM((3, 1, triple_count), jnp.int32),
-            pltpu.SemaphoreType.DMA((3,)),
+            pltpu.SemaphoreType.DMA((6,)),
             pltpu.SemaphoreType.DMA((chunks,)),
         ],
         interpret=interpret,
         name="count",
-    )(shot, pairs, triple_rows, events)
-    late_pairs, late_owners, _ = lax.optimization_barrier((pairs, owners, send))
-    table = pl.pallas_call(
-        functools.partial(table_kernel, shot_count=shot_count),
-        out_shape=jax.ShapeDtypeStruct((8, pair_count), jnp.int32),
-        in_specs=[smem()] * 4,
-        out_specs=smem(),
-        scratch_shapes=[pltpu.SMEM((shot_count,), jnp.int32)],
-        interpret=interpret,
-        name="table",
-    )(shot, panel, late_pairs, late_owners)
+    )(shot, panel, pairs, owners, triple_rows, events)
     other = lax.ppermute(send, SHOT[2], [(0, 1), (1, 0)])
     half = keep + other
     arrived = exchange(half.reshape(near, part, PB), SHOT[0])
@@ -337,9 +329,7 @@
     )(within(arrived.reshape(near * part, PB)))
     arrived = exchange(payload.reshape(far, own_rows, PB), SHOT[1])
     outgoing, rates, loads = pl.pallas_call(
-        functools.partial(
-            route_kernel, patches=patches, pair_count=pair_count, far=far, group=group, inverse=inverse
-        ),
+        functools.partial(route_kernel, patches=patches, pair_count=pair_count, far=far, group=group, inverse=inverse),
         out_shape=(near_f32(shot_count * SLOT_ROWS, PB), f32(2 * patches, PB), near_f32(1, PB)),
         in_specs=[smem(), vmem()],
         out_specs=(vmem(), vmem(), vmem()),

time: 82.8 us -> 81.4 us (0.983)
  blocking collectives: 45 us -> 61.1 us
  waiting for transfers between devices: 13.6 us -> 2.84 us
  starting transfers between devices: 11.8 us -> 8.36 us
  Pallas kernels: 11.2 us -> 7.9 us
    all_to_all x1 -> x2, blocking collectives: 23.4 us -> 38.8 us  [exchange(): return lax.all_to_all(x, axis, split_axis=0, concat_axis=0, tiled=True)]
    all_to_all x2 -> x1, waiting for transfers between devices: 10.7 us -> 0.01 us  [exchange(): return lax.all_to_all(x, axis, split_axis=0, concat_axis=0, tiled=True)]
    all_to_all x2 -> x1, starting transfers between devices: 9.86 us -> 6.44 us  [exchange(): return lax.all_to_all(x, axis, split_axis=0, concat_axis=0, tiled=True)]
    pallas_call x1 -> x0, Pallas kernels: 2.17 us -> none  [local(): pl.pallas_call(functools.partial(table_kernel, shot_count=shot_count), ou...]
  transfers between devices with their start and end apart: 3 -> 2, of which waited for: 2 -> 1; matrix products, arithmetic and copies ran while one was open for 0% -> 0% of each run, Pallas kernels for 3% -> 0%
where the time goes in v3:
time: 81.4 us; the launch traced here: 81 us
  blocking collectives  61.1 us (75%)
  starting transfers between devices  8.36 us (10%)
  Pallas kernels  7.9 us (10%)
  waiting for transfers between devices  2.84 us (3%)
    all_to_all x2, blocking collectives, exchange(): return lax.all_to_all(x, axis, split_axis=0, concat_axis=0, tiled=True)  38.8 us
    all_gather x1, blocking collectives, local(): panels = lax.all_gather(loads, 'det').reshape(det_count, PB)  22.3 us
    all_to_all x1, starting transfers between devices, exchange(): return lax.all_to_all(x, axis, split_axis=0, concat_axis=0, tiled=True)  6.44 us
    pallas_call x1, Pallas kernels, local(): pl.pallas_call(functools.partial(count_kernel, chunks=chunks, patches=pat...  5.32 us
    ppermute x1, waiting for transfers between devices, local(): other = lax.ppermute(send, SHOT[2], [(0, 1), (1, 0)])  2.84 us
    ppermute x1, starting transfers between devices, local(): other = lax.ppermute(send, SHOT[2], [(0, 1), (1, 0)])  1.92 us
    pallas_call x1, Pallas kernels, local(): pl.pallas_call(functools.partial(route_kernel, patches=patches, pair_coun...  1.73 us
  transfers between devices with their start and end apart: 2, of which 1 were waited for; matrix products, arithmetic and copies ran while one was open for 0% of the time, Pallas kernels for 0%

profile of v3, /device:TPU:6, one launch (start us, length us, event | category | flops | bytes accessed | tf_op | source)
XLA Modules:
  0.0 81.0 jit_solution(8081709156818170180)
XLA Ops:
  0.6 5.3 %count.1 = (f32[2336,128]{1,0:T(8,128)S(1)}, f32[2336,128]{1,0:T(8,128)S(1)}, s32[8,26]{1,0:T(8,128)}) custom-call(s32[1]{0:T(128)} %bitcast.shot_in, s32[1]{0:T(128)} %bitcast.1.panel_in, s32[2,26]{1,0:T(2,128)} %bitcast.26, s32[2,26]{1,0:T(2,128)} %bitcast.27, s32[3,1,256]{2,1,0:T(1,128)} %bitcast.25, s32[1024,1024]{1,0:T(8,128)} %events.1), custom_call_target="tpu_custom_call" | custom-call | tf_op jit(solution)/shard_map/count/pallas_call | solution.py:283
  6.0 1.9 %collective-permute-start = (f32[2336,128]{1,0:T(8,128)S(1)}, f32[2336,128]{1,0:T(8,128)S(1)}, u32[]{:S(2)}, u32[]{:S(2)}) collective-permute-start(f32[2336,128]{1,0:T(8,128)S(1)} %get-tuple-element.15), channel_id=1, source_target_pairs={{0,8},{8,0},{1,9},{9,1},{2,10},{10,2},{3,11},{11,3},{4,12},{12,4},... | collective-permute-start | bytes 3588104 | tf_op jit(solution)/shard_map/ppermute | solution.py:319
  7.9 2.8 %collective-permute-done = f32[2336,128]{1,0:T(8,128)S(1)} collective-permute-done((f32[2336,128]{1,0:T(8,128)S(1)}, f32[2336,128]{1,0:T(8,128)S(1)}, u32[]{:S(2)}, u32[]{:S(2)}) %collective-permute-start) | collective-permute-done | bytes 1196064 | tf_op jit(solution)/shard_map/ppermute | solution.py:319
  10.7 0.1 add.11
  10.9 23.4 %all_to_all.15 = f32[4,584,128]{2,1,0:T(8,128)S(1)} all-to-all(f32[4,584,128]{2,1,0:T(8,128)S(1)} %bitcast.24), channel_id=1, replica_groups=mesh['shot_0'=4,'shot_1'=8,'shot_2'=2,'det'=8] {'shot_0'}, dimensions={0} | all-to-all | bytes 2392064 | tf_op jit(solution)/shard_map/all_to_all | solution.py:259
  34.3 0.1 fold.1
  34.3 15.4 %all_to_all.16.arrived = f32[8,80,128]{2,1,0:T(8,128)S(1)} all-to-all(f32[8,80,128]{2,1,0:T(8,128)S(1)} %bitcast.20), channel_id=1, replica_groups=mesh['shot_0'=4,'shot_1'=8,'shot_2'=2,'det'=8] {'shot_1'}, dimensions={0} | all-to-all | bytes 655360 | tf_op jit(solution)/shard_map/all_to_all | solution.py:259
  49.7 1.7 %route.1 = (f32[512,128]{1,0:T(8,128)}, f32[16,128]{1,0:T(8,128)}, f32[1,128]{1,0:T(1,128)S(1)}) custom-call(s32[8,26]{1,0:T(8,128)} %get-tuple-element.13.table, f32[8,80,128]{2,1,0:T(8,128)S(1)} %all_to_all.16.arrived), custom_call_target="tpu_custom_call" | custom-call | tf_op jit(solution)/shard_map/route/pallas_call | solution.py:331
  51.5 6.4 %all-to-all-start.2 = ((f32[64,8,128]{2,1,0:T(8,128)}), f32[64,8,128]{2,1,0:T(8,128)S(1)}, u32[]{:S(2)}, u32[]{:S(2)}) async-start(f32[64,8,128]{2,1,0:T(8,128)} %bitcast.13), calls=%async_computation.2 | async-start | bytes 524288 | tf_op jit(solution)/shard_map/all_to_all | solution.py:259
  57.9 22.3 %all-gather.1 = f32[8,1,128]{2,1,0:T(1,128)S(1)} all-gather(f32[1,1,128]{2,1,0:T(1,128)S(1)} %bitcast.23), channel_id=2, replica_groups=mesh['shot_0'=4,'shot_1'=8,'shot_2'=2,'det'=8] {'det'}, dimensions={0}, use_global_device_ids=true | all-gather | bytes 4608 | tf_op jit(solution)/shard_map/all_gather | solution.py:346
  80.3 0.0 all-to-all-done.2
  80.3 0.8 owner.1
Async XLA Ops:
  6.0 4.8 %collective-permute-start = (f32[2336,128]{1,0:T(8,128)S(1)}, f32[2336,128]{1,0:T(8,128)S(1)}, u32[]{:S(2)}, u32[]{:S(2)}) collective-permute-start(f32[2336,128]{1,0:T(8,128)S(1)} %get-tuple-element.15), channel_id=1, source_target_pairs={{0,8},{8,0},{1,9},{9,1},{2,10},{10,2},{3,11},{11,3},{4,12},{12,4},... | collective-permute-start | bytes 3588104 | tf_op jit(solution)/shard_map/ppermute | solution.py:319
  51.5 28.8 %all-to-all-start.2 = ((f32[64,8,128]{2,1,0:T(8,128)}), f32[64,8,128]{2,1,0:T(8,128)S(1)}, u32[]{:S(2)}, u32[]{:S(2)}) async-start(f32[64,8,128]{2,1,0:T(8,128)} %bitcast.13), calls=%async_computation.2 | async-start | bytes 524288 | tf_op jit(solution)/shard_map/all_to_all | solution.py:259

commit v4 on v3

--- a/solution.py
+++ b/solution.py
@@ -149,7 +149,7 @@
     copy_table.wait()
 
 
-def fold_kernel(arrived, payload, *, near, far, rows_own, patches):
+def fold_kernel(arrived, payload, *, near, far, rows_own, own_rows, patches):
     part = far * rows_own + patches
 
     def total(start, rows):
@@ -160,9 +160,11 @@
 
     counts = total(far * rows_own, patches)
     for y in range(far):
-        row = y * (rows_own + patches)
+        row = y * own_rows
         payload[row : row + rows_own, :] = total(y * rows_own, rows_own)
         payload[row + rows_own : row + rows_own + patches, :] = counts
+        rest = own_rows - rows_own - patches
+        payload[row + own_rows - rest : row + own_rows, :] = jnp.zeros((rest, PB), jnp.float32)
 
 
 def route_kernel(
@@ -174,12 +176,12 @@
         total += arrived[y]
     own[...] = total
     vector_row = 2 * (patches + pair_count)
-    counts_row = total.shape[0] - patches
+    counts_row = vector_row + 2
     first = 2 * table[6, 0]
     lines = 2 * patches
     lane = iota((lines, PB), 1)
     line = iota((lines, PB), 0)
-    counts = own[counts_row:, :]
+    counts = own[counts_row : counts_row + patches, :]
     both = jnp.concatenate([counts, counts], axis=0)
     mine = jnp.sum(jnp.where(lane == first + line // patches, both, 0.0), axis=1, keepdims=True)
     rates[:lines, :] = jnp.broadcast_to(mine, (lines, PB))
@@ -275,8 +277,8 @@
     triple_rows = triples.transpose(2, 0, 1)
     triple_count = triple_rows.shape[2]
     group = triple_count // far
-    rows_own = 2 * (patches + pair_count) + 4
-    own_rows = rows_own + patches
+    rows_own = 2 * (patches + pair_count) + 2
+    own_rows = -(-(rows_own + patches) // 8) * 8
     part = far * rows_own + patches
     chunks = 4
 
@@ -320,7 +322,9 @@
     half = keep + other
     arrived = exchange(half.reshape(near, part, PB), SHOT[0])
     payload = pl.pallas_call(
-        functools.partial(fold_kernel, near=near, far=far, rows_own=rows_own, patches=patches),
+        functools.partial(
+            fold_kernel, near=near, far=far, rows_own=rows_own, own_rows=own_rows, patches=patches
+        ),
         out_shape=near_f32(far * own_rows, PB),
         in_specs=[vmem()],
         out_specs=vmem(),

time: 81.4 us -> 80.5 us (0.989)
  no operation moved by 1% of the time
where the time goes in v4:
time: 80.5 us; the launch traced here: 80.1 us
  blocking collectives  60.5 us (75%)
  starting transfers between devices  8.36 us (10%)
  Pallas kernels  7.7 us (10%)
  waiting for transfers between devices  2.79 us (3%)
    all_to_all x2, blocking collectives, exchange(): return lax.all_to_all(x, axis, split_axis=0, concat_axis=0, tiled=True)  38.5 us
    all_gather x1, blocking collectives, local(): panels = lax.all_gather(loads, 'det').reshape(det_count, PB)  22 us
    all_to_all x1, starting transfers between devices, exchange(): return lax.all_to_all(x, axis, split_axis=0, concat_axis=0, tiled=True)  6.44 us
    pallas_call x1, Pallas kernels, local(): pl.pallas_call(functools.partial(count_kernel, chunks=chunks, patches=pat...  5.12 us
    ppermute x1, waiting for transfers between devices, local(): other = lax.ppermute(send, SHOT[2], [(0, 1), (1, 0)])  2.79 us
    ppermute x1, starting transfers between devices, local(): other = lax.ppermute(send, SHOT[2], [(0, 1), (1, 0)])  1.92 us
    pallas_call x1, Pallas kernels, local(): pl.pallas_call(functools.partial(route_kernel, patches=patches, pair_coun...  1.73 us
  transfers between devices with their start and end apart: 2, of which 1 were waited for; matrix products, arithmetic and copies ran while one was open for 0% of the time, Pallas kernels for 0%

profile of v4, /device:TPU:6, one launch (start us, length us, event | category | flops | bytes accessed | tf_op | source)
XLA Modules:
  0.0 80.1 jit_solution(5563187882256788209)
XLA Ops:
  0.6 5.1 %count.1 = (f32[2272,128]{1,0:T(8,128)S(1)}, f32[2272,128]{1,0:T(8,128)S(1)}, s32[8,26]{1,0:T(8,128)}) custom-call(s32[1]{0:T(128)} %bitcast.shot_in, s32[1]{0:T(128)} %bitcast.1.panel_in, s32[2,26]{1,0:T(2,128)} %bitcast.26, s32[2,26]{1,0:T(2,128)} %bitcast.27, s32[3,1,256]{2,1,0:T(1,128)} %bitcast.25, s32[1024,1024]{1,0:T(8,128)} %events.1), custom_call_target="tpu_custom_call" | custom-call | tf_op jit(solution)/shard_map/count/pallas_call | solution.py:285
  5.8 1.9 %collective-permute-start = (f32[2272,128]{1,0:T(8,128)S(1)}, f32[2272,128]{1,0:T(8,128)S(1)}, u32[]{:S(2)}, u32[]{:S(2)}) collective-permute-start(f32[2272,128]{1,0:T(8,128)S(1)} %get-tuple-element.15), channel_id=1, source_target_pairs={{0,8},{8,0},{1,9},{9,1},{2,10},{10,2},{3,11},{11,3},{4,12},{12,4},... | collective-permute-start | bytes 3489800 | tf_op jit(solution)/shard_map/ppermute | solution.py:321
  7.7 2.8 %collective-permute-done = f32[2272,128]{1,0:T(8,128)S(1)} collective-permute-done((f32[2272,128]{1,0:T(8,128)S(1)}, f32[2272,128]{1,0:T(8,128)S(1)}, u32[]{:S(2)}, u32[]{:S(2)}) %collective-permute-start) | collective-permute-done | bytes 1163296 | tf_op jit(solution)/shard_map/ppermute | solution.py:321
  10.5 0.1 add.11
  10.6 23.1 %all_to_all.15 = f32[4,568,128]{2,1,0:T(8,128)S(1)} all-to-all(f32[4,568,128]{2,1,0:T(8,128)S(1)} %bitcast.24), channel_id=1, replica_groups=mesh['shot_0'=4,'shot_1'=8,'shot_2'=2,'det'=8] {'shot_0'}, dimensions={0} | all-to-all | bytes 2326528 | tf_op jit(solution)/shard_map/all_to_all | solution.py:261
  33.7 0.1 fold.1
  33.7 15.4 %all_to_all.16.arrived = f32[8,80,128]{2,1,0:T(8,128)S(1)} all-to-all(f32[8,80,128]{2,1,0:T(8,128)S(1)} %bitcast.20), channel_id=1, replica_groups=mesh['shot_0'=4,'shot_1'=8,'shot_2'=2,'det'=8] {'shot_1'}, dimensions={0} | all-to-all | bytes 655360 | tf_op jit(solution)/shard_map/all_to_all | solution.py:261
  49.1 1.7 %route.1 = (f32[512,128]{1,0:T(8,128)}, f32[16,128]{1,0:T(8,128)}, f32[1,128]{1,0:T(1,128)S(1)}) custom-call(s32[8,26]{1,0:T(8,128)} %get-tuple-element.13.table, f32[8,80,128]{2,1,0:T(8,128)S(1)} %all_to_all.16.arrived), custom_call_target="tpu_custom_call" | custom-call | tf_op jit(solution)/shard_map/route/pallas_call | solution.py:335
  50.9 6.4 %all-to-all-start.2 = ((f32[64,8,128]{2,1,0:T(8,128)}), f32[64,8,128]{2,1,0:T(8,128)S(1)}, u32[]{:S(2)}, u32[]{:S(2)}) async-start(f32[64,8,128]{2,1,0:T(8,128)} %bitcast.13), calls=%async_computation.2 | async-start | bytes 524288 | tf_op jit(solution)/shard_map/all_to_all | solution.py:261
  57.3 22.0 %all-gather.1 = f32[8,1,128]{2,1,0:T(1,128)S(1)} all-gather(f32[1,1,128]{2,1,0:T(1,128)S(1)} %bitcast.23), channel_id=2, replica_groups=mesh['shot_0'=4,'shot_1'=8,'shot_2'=2,'det'=8] {'det'}, dimensions={0}, use_global_device_ids=true | all-gather | bytes 4608 | tf_op jit(solution)/shard_map/all_gather | solution.py:350
  79.4 0.0 all-to-all-done.2
  79.4 0.8 owner.1
Async XLA Ops:
  5.8 4.7 %collective-permute-start = (f32[2272,128]{1,0:T(8,128)S(1)}, f32[2272,128]{1,0:T(8,128)S(1)}, u32[]{:S(2)}, u32[]{:S(2)}) collective-permute-start(f32[2272,128]{1,0:T(8,128)S(1)} %get-tuple-element.15), channel_id=1, source_target_pairs={{0,8},{8,0},{1,9},{9,1},{2,10},{10,2},{3,11},{11,3},{4,12},{12,4},... | collective-permute-start | bytes 3489800 | tf_op jit(solution)/shard_map/ppermute | solution.py:321
  50.9 28.5 %all-to-all-start.2 = ((f32[64,8,128]{2,1,0:T(8,128)}), f32[64,8,128]{2,1,0:T(8,128)S(1)}, u32[]{:S(2)}, u32[]{:S(2)}) async-start(f32[64,8,128]{2,1,0:T(8,128)} %bitcast.13), calls=%async_computation.2 | async-start | bytes 524288 | tf_op jit(solution)/shard_map/all_to_all | solution.py:261
